TPU v7x, 256 devices: a whole 4x4x8 slice. The times are simulated.
256 devices in a mesh: row: 8 (over y_hi, x), col: 32 (over z, y_lo, core).
Axes of the slice: x: 4, y: 4 (y_hi: 2, y_lo: 2; y = y_hi * 2 + y_lo), z: 8, core: 2. Of those that a mesh axis runs over, the one named last changes fastest.
Arguments:
- gradient: bfloat16 [2304, 18432], P('row', 'col'), may hold values from -6 to 6
- left_basis: bfloat16 [2304, 2304], P('row'), may hold values from -0.125 to 0.125
- right_basis: bfloat16 [18432, 18432], P('col', 'row'), may hold values from -0.046875 to 0.046875
- first_moment: float32 [2304, 18432], P('col', 'row'), may hold values from -3 to 3
- second_moment: float32 [2304, 18432], P('col', 'row'), may hold values from 0.25 to 4
Outputs:
- update: bfloat16 [2304, 18432], P('row', 'col')
- first_new: float32 [2304, 18432], P('col', 'row')
- second_new: float32 [2304, 18432], P('col', 'row')
All inputs are finite; a program needn't handle non-finite values.
Results may differ from a plain program's by a relative error of at most 0.018.
Values may be sent and summed in bfloat16 or wider, within the bound.
No kernel may reach another device: no remote copies, remote signals or barrier semaphores. Data moves between devices by JAX's collectives and lax.ppermute only.
A program may use at most 64 MiB of HBM per device.

v0:
```python
import jax
import jax.numpy as jnp
from jax import lax
from jax.sharding import PartitionSpec as P

beta_one = 0.9
beta_two = 0.95
epsilon = 1e-08
correct_one = 1.0 - 0.9**10
correct_two = 1.0 - 0.95**10


def cut_along(shard, dim, size):
    before, after = (shard.shape[:dim], shard.shape[dim + 1 :])
    return jnp.moveaxis(shard.reshape(*before, size, -1, *after), dim, 0)


def sum_at_owner(shard, axis, dim):
    size = lax.axis_size(axis)
    blocks = lax.all_to_all(cut_along(shard, dim, size), axis, 0, 0, tiled=True)
    return jnp.sum(blocks.astype(jnp.float32), axis=0)


def copy_for_each(shard, axis):
    copies = jnp.broadcast_to(shard, (lax.axis_size(axis), *shard.shape))
    return lax.all_to_all(copies, axis, split_axis=0, concat_axis=0, tiled=True)


def in_order(blocks, dim):
    blocks = jnp.moveaxis(blocks, 0, dim)
    dims = blocks.shape
    return blocks.reshape(*dims[:dim], dims[dim] * dims[dim + 1], *dims[dim + 2 :])


def gathered_copies(shard, axis, dim):
    blocks = copy_for_each(shard, axis)
    return in_order(blocks, dim)


def per_device(gradient, left_basis, right_basis, first_moment, second_moment):
    partial_value = lax.dot_general(
        left_basis, gradient, (((0,), (0,)), ((), ())), preferred_element_type=jnp.float32
    )
    rotated_left = lax.psum(partial_value.astype(jnp.bfloat16), "row")
    rotated = lax.psum_scatter(
        jnp.dot(rotated_left, right_basis, preferred_element_type=jnp.float32).astype(jnp.bfloat16),
        "col",
        scatter_dimension=0,
        tiled=True,
    )
    rotated_wide = rotated.astype(jnp.float32)
    first_new = beta_one * first_moment + (1.0 - beta_one) * rotated_wide
    second_new = beta_two * second_moment + (1.0 - beta_two) * rotated_wide * rotated_wide
    step_rot = (first_new / correct_one / (jnp.sqrt(second_new / correct_two) + epsilon)).astype(
        jnp.bfloat16
    )
    back_part = lax.dot_general(
        lax.all_gather(step_rot, "col", axis=0, tiled=True),
        right_basis,
        (((1,), (1,)), ((), ())),
        preferred_element_type=jnp.float32,
    )
    back_own = sum_at_owner(back_part.astype(jnp.bfloat16), "row", 0).astype(jnp.bfloat16)
    back_rot = gathered_copies(back_own, "row", 0)
    update = jnp.dot(left_basis, back_rot, preferred_element_type=jnp.float32).astype(jnp.bfloat16)
    return (update, first_new, second_new)


def solution(mesh):
    in_specs = (P("row", "col"), P("row", None), P("col", "row"), P("col", "row"), P("col", "row"))
    out_specs = (P("row", "col"), P("col", "row"), P("col", "row"))
    return jax.shard_map(
        per_device, mesh=mesh, in_specs=in_specs, out_specs=out_specs, check_vma=False
    )
```

profile of v0, /device:TPU:32, one launch (start us, length us, event | category | flops | bytes accessed | tf_op | source)
XLA Modules:
  0.0 455.3 jit_solution(5712850803293261897)
XLA Ops:
  7.2 0.0 copy-start
  7.2 0.0 all-reduce.2.cloned.1.call-start
  7.2 5.1 %convolution_convert_fusion.1 = bf16[2304,576]{1,0:T(8,128)(2,1)} fusion(bf16[288,2304]{1,0:T(8,128)(2,1)} %param.6, bf16[288,576]{1,0:T(8,128)(2,1)} %param.5), kind=kOutput, calls=%fused_computation.1 | convolution fusion | flops 765739008 | bytes 4313088 | tf_op jit(solution)/shard_map/dot_general | solution.py:41
  12.3 0.0 all-reduce.2.cloned.1.call-update
  12.3 0.0 reduce-scatter.2.cloned.1.call-start
  12.4 106.2 %all-reduce.2.cloned.1.call-done = bf16[2304,576]{1,0:T(8,128)(2,1)} async-done(((bf16[2304,576]{1,0:T(8,128)(2,1)}), bf16[2304,576]{1,0:T(8,128)(2,1)}) %all-reduce.2.cloned.1.call-update) | async-done | bytes 2654224 | tf_op jit(solution)/shard_map/psum | solution.py:44
  118.6 0.0 copy-done
  118.6 12.5 %convolution_convert_fusion = bf16[2304,2304]{1,0:T(8,128)(2,1)} fusion(bf16[2304,576]{1,0:T(8,128)(2,1)} %all-reduce.2.cloned.1.call-done, bf16[576,2304]{1,0:T(8,128)(2,1)S(1)} %copy-done), kind=kOutput, calls=%fused_computation | convolution fusion | flops 6120603648 | bytes 15925248 | tf_op jit(solution)/shard_map/dot_general | solution.py:46
  131.0 0.0 copy-start.1
  131.1 0.0 reduce-scatter.2.cloned.1.call-update
  131.1 0.0 all-gather.2.cloned.1.call-start
  131.1 129.7 %reduce-scatter.2.cloned.1.call-done = bf16[72,2304]{1,0:T(8,128)(2,1)} async-done(((bf16[2304,2304]{1,0:T(8,128)(2,1)}), bf16[72,2304]{1,0:T(8,128)(2,1)}) %reduce-scatter.2.cloned.1.call-update) | async-done | bytes 331792 | tf_op jit(solution)/shard_map/reduce_scatter | solution.py:45
  260.9 0.0 copy-done.1
  260.9 2.6 divide_convert_fusion
  263.4 0.0 all-gather.2.cloned.1.call-update
  263.5 79.1 %all-gather.2.cloned.1.call-done = bf16[2304,2304]{1,0:T(8,128)(2,1)} async-done(((bf16[72,2304]{1,0:T(8,128)(2,1)}), bf16[2304,2304]{1,0:T(8,128)(2,1)}) %all-gather.2.cloned.1.call-update) | async-done | bytes 10616848 | tf_op jit(solution)/shard_map/all_gather | solution.py:58
  342.5 11.7 %convolution_convert_fusion.2 = bf16[2304,576]{0,1:T(8,128)(2,1)} fusion(bf16[2304,2304]{1,0:T(8,128)(2,1)} %all-gather.2.cloned.1.call-done, bf16[576,2304]{1,0:T(8,128)(2,1)S(1)} %copy-done), kind=kOutput, calls=%fused_computation.2 | convolution fusion | flops 6116622336 | bytes 15925248 | tf_op jit(solution)/shard_map/dot_general | solution.py:57
  354.3 4.5 copy.8
  358.8 44.9 %all_to_all.10 = bf16[8,288,576]{2,1,0:T(8,128)(2,1)} all-to-all(bf16[8,288,576]{2,1,0:T(8,128)(2,1)} %bitcast.12), channel_id=1, replica_groups=mesh['row'=8,'col'=32] {'row'}, dimensions={0} | all-to-all | bytes 5308416 | tf_op jit(solution)/shard_map/all_to_all | solution.py:20
  403.7 2.4 reduce_sum.12
  406.1 0.2 broadcast_in_dim.3
  406.3 0.0 copy-start.2
  406.3 40.5 %all_to_all.11 = bf16[8,288,576]{2,1,0:T(8,128)(2,1)S(1)} all-to-all(bf16[8,288,576]{2,1,0:T(8,128)(2,1)S(1)} %broadcast_in_dim.3), channel_id=1, replica_groups=mesh['row'=8,'col'=32] {'row'}, dimensions={0} | all-to-all | bytes 5308416 | tf_op jit(solution)/shard_map/all_to_all | solution.py:26
  446.8 0.0 copy-done.2
  446.8 1.9 fusion
Async XLA Ops:
  7.2 111.4 %copy-start = (bf16[576,2304]{1,0:T(8,128)(2,1)S(1)}, bf16[576,2304]{1,0:T(8,128)(2,1)}, u32[]{:S(2)}) copy-start(bf16[576,2304]{1,0:T(8,128)(2,1)} %param.7) | copy-start | bytes 7962628
  7.2 111.4 %all-reduce.2.cloned.1.call-start = ((), (), s32[]{:S(2)}) async-start(), calls=%async_computation.3 | async-start | bytes 5898240 | tf_op jit(solution)/shard_map/psum | solution.py:44
  12.3 248.6 %reduce-scatter.2.cloned.1.call-start = ((), (), s32[]{:S(2)}) async-start(), calls=%async_computation.4 | async-start | bytes 10948608 | tf_op jit(solution)/shard_map/reduce_scatter | solution.py:45
  131.0 129.8 %copy-start.1 = (f32[72,2304]{1,0:T(8,128)S(1)}, f32[72,2304]{1,0:T(8,128)}, u32[]{:S(2)}) copy-start(f32[72,2304]{1,0:T(8,128)} %param.8) | copy-start | bytes 1990660
  131.1 211.4 %all-gather.2.cloned.1.call-start = ((), (), s32[]{:S(2)}) async-start(), calls=%async_computation.5 | async-start | bytes 10948608 | tf_op jit(solution)/shard_map/all_gather | solution.py:58
  406.3 40.5 %copy-start.2 = (bf16[288,2304]{1,0:T(8,128)(2,1)S(1)}, bf16[288,2304]{1,0:T(8,128)(2,1)}, u32[]{:S(2)}) copy-start(bf16[288,2304]{1,0:T(8,128)(2,1)} %param.6) | copy-start | bytes 3981316
Sparse Core Ops, SparseCore 0:
  12.4 106.1 all-reduce.1
  131.2 129.6 reduce-scatter.1
  263.6 78.8 all-gather.1
where the time goes:
time: 456 us; the launch traced here: 455 us
  waiting for transfers between devices  315 us (69%)
  blocking collectives  85.4 us (19%)
  matrix products  31.2 us (7%)
  between operations  13.8 us (3%)
  other arithmetic  4.99 us (1%)
  local copies, waits for them, and re-layouts  4.76 us (1%)
    reduce_scatter x1, waiting for transfers between devices, per_device(): lax.psum_scatter(jnp.dot(rotated_left, right_basis, preferred_element_typ...  130 us
    psum x1, waiting for transfers between devices, per_device(): rotated_left = lax.psum(partial_value.astype(jnp.bfloat16), 'row')  106 us
    all_gather x1, waiting for transfers between devices, per_device(): lax.all_gather(step_rot, 'col', axis=0, tiled=True)  79.1 us
    all_to_all x1, blocking collectives, sum_at_owner(): blocks = lax.all_to_all(cut_along(shard, dim, size), axis, 0, 0, tiled=True)  44.9 us
    all_to_all x1, blocking collectives, copy_for_each(): return lax.all_to_all(copies, axis, split_axis=0, concat_axis=0, tiled=True)  40.5 us
    dot_general x1, matrix products, per_device(): jnp.dot(rotated_left, right_basis, preferred_element_type=jnp.float32)  12.5 us
    dot_general x1, matrix products, per_device(): lax.dot_general(lax.all_gather(step_rot, 'col', axis=0, tiled=True), righ...  11.7 us
  transfers between devices with their start and end apart: 3, of which 3 were waited for; matrix products, arithmetic and copies ran while one was open for 0% of the time, Pallas kernels for 0%

commit v1 on v0

--- a/solution.py
+++ b/solution.py
@@ -41,7 +41,7 @@
     partial_value = lax.dot_general(
         left_basis, gradient, (((0,), (0,)), ((), ())), preferred_element_type=jnp.float32
     )
-    rotated_left = lax.psum(partial_value.astype(jnp.bfloat16), "row")
+    rotated_left = jnp.sum(lax.all_gather(partial_value.astype(jnp.bfloat16), "row"), axis=0)
     rotated = lax.psum_scatter(
         jnp.dot(rotated_left, right_basis, preferred_element_type=jnp.float32).astype(jnp.bfloat16),
         "col",

time: 456 us -> 643 us (1.41)
  waiting for transfers between devices: 315 us -> 442 us
  other arithmetic: 4.99 us -> 51.4 us
  local copies, waits for them, and re-layouts: 4.76 us -> 21.1 us
    all_gather x0 -> x1, waiting for transfers between devices: none -> 233 us  [per_device(): lax.all_gather(partial_value.astype(jnp.bfloat16), 'row')]
    psum x1 -> x0, waiting for transfers between devices: 106 us -> none  [per_device(): rotated_left = lax.psum(partial_value.astype(jnp.bfloat16), 'row')]
    reduce_sum x0 -> x1, other arithmetic: none -> 46.4 us  [per_device(): jnp.sum(lax.all_gather(partial_value.astype(jnp.bfloat16), 'row'), axis=0)]
    unnamed x6 -> x7, local copies, waits for them, and re-layouts: 0.02 us -> 16.3 us
where the time goes in v1:
time: 643 us
  waiting for transfers between devices  442 us (69%)
  blocking collectives  85.4 us (13%)
  other arithmetic  51.4 us (8%)
  matrix products  29.1 us (5%)
  local copies, waits for them, and re-layouts  21.1 us (3%)
  between operations  13.8 us (2%)
    all_gather x1, waiting for transfers between devices, per_device(): lax.all_gather(partial_value.astype(jnp.bfloat16), 'row')  233 us
    reduce_scatter x1, waiting for transfers between devices, per_device(): lax.psum_scatter(jnp.dot(rotated_left, right_basis, preferred_element_typ...  130 us
    all_gather x1, waiting for transfers between devices, per_device(): lax.all_gather(step_rot, 'col', axis=0, tiled=True)  77.9 us
    reduce_sum x1, other arithmetic, per_device(): jnp.sum(lax.all_gather(partial_value.astype(jnp.bfloat16), 'row'), axis=0)  46.4 us
    all_to_all x1, blocking collectives, sum_at_owner(): blocks = lax.all_to_all(cut_along(shard, dim, size), axis, 0, 0, tiled=True)  44.9 us
    all_to_all x1, blocking collectives, copy_for_each(): return lax.all_to_all(copies, axis, split_axis=0, concat_axis=0, tiled=True)  40.5 us
    unnamed x7, local copies, waits for them, and re-layouts  16.3 us
  transfers between devices with their start and end apart: 3, of which 3 were waited for; matrix products, arithmetic and copies ran while one was open for 0% of the time, Pallas kernels for 0%

profile of v1, /device:TPU:32, one launch (start us, length us, event | category | flops | bytes accessed | tf_op | source)
XLA Modules:
  0.0 642.7 jit_solution(6905320311075488674)
XLA Ops:
  7.2 0.0 copy-start
  7.2 0.0 all-gather.6.cloned.1.call-start
  7.2 4.6 convolution_convert_fusion.2
  11.9 0.0 all-gather.6.cloned.1.call-update
  11.9 0.0 reduce-scatter.2.cloned.1.call-start
  11.9 233.4 %all-gather.6.cloned.1.call-done = bf16[18432,576]{0,1:T(8,128)(2,1)} async-done(((bf16[2304,576]{0,1:T(8,128)(2,1)}), bf16[18432,576]{0,1:T(8,128)(2,1)}) %all-gather.6.cloned.1.call-update) | async-done | bytes 21233680 | tf_op jit(solution)/shard_map/all_gather | solution.py:44
  245.3 16.3 %copy.10 = bf16[72,8,8,2304]{3,2,1,0:T(8,128)(2,1)} copy(bf16[72,8,8,2304]{3,1,2,0:T(8,128)(2,1)} %bitcast.17) | data formatting | bytes 42467328
  261.6 46.4 %bitcast_reduce_fusion = bf16[2304,576]{0,1:T(8,128)(2,1)S(1)} fusion(bf16[72,8,8,2304]{3,2,1,0:T(8,128)(2,1)} %copy.10), kind=kLoop, calls=%fused_computation | loop fusion | flops 9289728 | bytes 23887872 | tf_op jit(solution)/shard_map/reduce_sum | solution.py:44
  308.1 0.0 copy-done
  308.1 10.8 %convolution_convert_fusion = bf16[2304,2304]{1,0:T(8,128)(2,1)} fusion(bf16[2304,576]{0,1:T(8,128)(2,1)S(1)} %bitcast_reduce_fusion, bf16[576,2304]{1,0:T(8,128)(2,1)S(1)} %copy-done), kind=kOutput, calls=%fused_computation.1 | convolution fusion | flops 6120603648 | bytes 15925248 | tf_op jit(solution)/shard_map/dot_general | solution.py:46
  318.9 0.0 copy-start.1
  318.9 0.0 reduce-scatter.2.cloned.1.call-update
  318.9 0.2 all-gather.4.cloned.1.call-start
  319.2 130.2 %reduce-scatter.2.cloned.1.call-done = bf16[72,2304]{1,0:T(8,128)(2,1)} async-done(((bf16[2304,2304]{1,0:T(8,128)(2,1)}), bf16[72,2304]{1,0:T(8,128)(2,1)}) %reduce-scatter.2.cloned.1.call-update) | async-done | bytes 331792 | tf_op jit(solution)/shard_map/reduce_scatter | solution.py:45
  449.4 0.0 copy-done.1
  449.4 2.6 divide_convert_fusion
  452.0 0.0 all-gather.4.cloned.1.call-update
  452.0 77.9 %all-gather.4.cloned.1.call-done = bf16[2304,2304]{1,0:T(8,128)(2,1)} async-done(((bf16[72,2304]{1,0:T(8,128)(2,1)}), bf16[2304,2304]{1,0:T(8,128)(2,1)}) %all-gather.4.cloned.1.call-update) | async-done | bytes 10616848 | tf_op jit(solution)/shard_map/all_gather | solution.py:58
  529.9 11.7 %convolution_convert_fusion.1 = bf16[2304,576]{0,1:T(8,128)(2,1)} fusion(bf16[2304,2304]{1,0:T(8,128)(2,1)} %all-gather.4.cloned.1.call-done, bf16[576,2304]{1,0:T(8,128)(2,1)S(1)} %copy-done), kind=kOutput, calls=%fused_computation.2 | convolution fusion | flops 6116622336 | bytes 15925248 | tf_op jit(solution)/shard_map/dot_general | solution.py:57
  541.6 4.5 copy.9
  546.1 44.9 %all_to_all.10 = bf16[8,288,576]{2,1,0:T(8,128)(2,1)} all-to-all(bf16[8,288,576]{2,1,0:T(8,128)(2,1)} %bitcast.18), channel_id=1, replica_groups=mesh['row'=8,'col'=32] {'row'}, dimensions={0} | all-to-all | bytes 5308416 | tf_op jit(solution)/shard_map/all_to_all | solution.py:20
  591.0 2.4 reduce_sum.25
  593.4 0.2 broadcast_in_dim.3
  593.7 0.0 copy-start.2
  593.7 40.5 %all_to_all.11 = bf16[8,288,576]{2,1,0:T(8,128)(2,1)S(1)} all-to-all(bf16[8,288,576]{2,1,0:T(8,128)(2,1)S(1)} %broadcast_in_dim.3), channel_id=1, replica_groups=mesh['row'=8,'col'=32] {'row'}, dimensions={0} | all-to-all | bytes 5308416 | tf_op jit(solution)/shard_map/all_to_all | solution.py:26
  634.2 0.0 copy-done.2
  634.2 1.9 fusion
Async XLA Ops:
  7.2 300.9 %copy-start = (bf16[576,2304]{1,0:T(8,128)(2,1)S(1)}, bf16[576,2304]{1,0:T(8,128)(2,1)}, u32[]{:S(2)}) copy-start(bf16[576,2304]{1,0:T(8,128)(2,1)} %param.7) | copy-start | bytes 7962628
  7.2 238.1 %all-gather.6.cloned.1.call-start = ((), (), s32[]{:S(2)}) async-start(), calls=%async_computation.5 | async-start | bytes 23887872 | tf_op jit(solution)/shard_map/all_gather | solution.py:44
  11.9 437.5 %reduce-scatter.2.cloned.1.call-start = ((), (), s32[]{:S(2)}) async-start(), calls=%async_computation.3 | async-start | bytes 10948608 | tf_op jit(solution)/shard_map/reduce_scatter | solution.py:45
  318.9 130.5 %copy-start.1 = (f32[72,2304]{1,0:T(8,128)S(1)}, f32[72,2304]{1,0:T(8,128)}, u32[]{:S(2)}) copy-start(f32[72,2304]{1,0:T(8,128)} %param.8) | copy-start | bytes 1990660
  318.9 211.0 %all-gather.4.cloned.1.call-start = ((), (), s32[]{:S(2)}) async-start(), calls=%async_computation.4 | async-start | bytes 10948608 | tf_op jit(solution)/shard_map/all_gather | solution.py:58
  593.7 40.5 %copy-start.2 = (bf16[288,2304]{1,0:T(8,128)(2,1)S(1)}, bf16[288,2304]{1,0:T(8,128)(2,1)}, u32[]{:S(2)}) copy-start(bf16[288,2304]{1,0:T(8,128)(2,1)} %param.6) | copy-start | bytes 3981316
Sparse Core Ops, SparseCore 0:
  12.0 233.2 all-gather.5
  319.1 130.2 reduce-scatter.1
  452.1 77.7 all-gather.3
